TPU v7x, 32 devices: a whole 2x2x4 slice. The times are simulated.
32 devices in a mesh: prow: 4 (over y, x), pcol: 8 (over z, core).
Axes of the slice: x: 2, y: 2, z: 4, core: 2. Of those that a mesh axis runs over, the one named last changes fastest.
Arguments:
- inverse_factor: float32 [1024, 1024], P('pcol'), as said below
- diag_block: float32 [1024, 1024], P('pcol'), as said below
- panel_matrix: float32 [16, 4, 128, 1024], P(None, 'prow', 'pcol'), may hold values from -6 to 6
- panel_factor: float32 [16, 4, 128, 1024], P(None, 'prow', 'pcol'), may hold values from -0.1875 to 0.1875
- trailing: float32 [16, 4, 128, 8, 8, 128], P(None, 'prow', None, None, 'pcol'), may hold values from -6 to 6
Outputs:
- reduced_diag: float32 [1024, 1024], P('pcol')
- panel_result: float32 [16, 4, 128, 1024], P(None, 'prow', 'pcol')
- trailing_out: float32 [16, 4, 128, 8, 8, 128], P(None, 'prow', None, None, 'pcol')
Inputs may be any that keep to these rules, and one draw needn't show every extreme that they name: `inverse_factor`: lower triangular, diagonal entries between 0.5 and 2. `diag_block`: symmetric.
All inputs are finite; a program needn't handle non-finite values.
Results may differ from a plain program's by a relative error of at most 0.0003.
Values sent between devices are 32-bit elements; how exact they have to be, the bound alone decides.
A program may use at most 128 MiB of HBM per device.

v0:
```python
import jax
import jax.numpy as jnp
from jax import lax
from jax.sharding import PartitionSpec as P


def broadcast(array, axis, root):
    mine = lax.axis_index(axis) == root
    return lax.psum(jnp.where(mine, array, jnp.zeros_like(array)), axis)


def body(inverse_factor, diag_block, panel_matrix, panel_factor, trailing):
    exact = lax.Precision.HIGHEST
    grid_rows = lax.axis_size("prow")
    grid_cols = lax.axis_size("pcol")
    column = lax.axis_index("pcol")
    grid_row = lax.axis_index("prow")
    local_rows = inverse_factor.shape[0]
    width = inverse_factor.shape[1]
    inverse_full = lax.all_gather(inverse_factor, "pcol", axis=0, tiled=True)
    diag_terms = jnp.dot(
        diag_block, inverse_full.T, precision=exact, preferred_element_type=jnp.float32
    )
    terms_full = lax.all_gather(diag_terms, "pcol", axis=0, tiled=True)
    reduced = jnp.dot(inverse_full, terms_full, precision=exact, preferred_element_type=jnp.float32)
    reduced_rows = lax.dynamic_slice_in_dim(reduced, column * local_rows, local_rows, 0)
    shape = panel_matrix.shape
    solved = jnp.dot(
        panel_matrix.reshape(-1, width),
        inverse_full.T,
        precision=exact,
        preferred_element_type=jnp.float32,
    )
    coupled = jnp.dot(
        panel_factor.reshape(-1, width),
        reduced,
        precision=exact,
        preferred_element_type=jnp.float32,
    )
    shifted = solved - 0.5 * coupled
    panel_result = (shifted - 0.5 * coupled).reshape(shape)
    rows_y, rows_l = (
        lax.all_gather(shifted.reshape(shape), "pcol", axis=2, tiled=True),
        lax.all_gather(panel_factor, "pcol", axis=2, tiled=True),
    )
    tile_rows = rows_y.shape[0]
    tile = rows_y.shape[2]
    col_tiles = trailing.shape[3]
    stride = grid_cols // grid_rows
    picked = column // grid_rows

    def select(rows):
        grouped = rows.reshape(col_tiles, stride, tile, width)
        return lax.dynamic_index_in_dim(grouped, picked, 1, keepdims=False)

    col_y, col_l = (
        broadcast(select(rows_y), "prow", column % grid_rows),
        broadcast(select(rows_l), "prow", column % grid_rows),
    )
    rows_y = rows_y.reshape(tile_rows, tile, width)
    rows_l = rows_l.reshape(tile_rows, tile, width)
    block = trailing.reshape(tile_rows, tile, col_tiles, tile)
    row_ids = jnp.arange(tile_rows, dtype=jnp.int32) * grid_rows + grid_row
    col_ids = jnp.arange(col_tiles, dtype=jnp.int32) * grid_cols + column
    lower = (row_ids[:, None] >= col_ids[None, :])[:, None, :, None]
    update = jnp.einsum(
        "isk,jtk->isjt", rows_y, col_l, precision=exact, preferred_element_type=jnp.float32
    )
    update = update + jnp.einsum(
        "isk,jtk->isjt", rows_l, col_y, precision=exact, preferred_element_type=jnp.float32
    )
    result = jnp.where(lower, block - update, block)
    return (reduced_rows, panel_result, result.reshape(trailing.shape))


def solution(mesh):
    in_specs = (
        P("pcol", None),
        P("pcol", None),
        P(None, "prow", "pcol", None),
        P(None, "prow", "pcol", None),
        P(None, "prow", None, None, "pcol", None),
    )
    out_specs = (
        P("pcol", None),
        P(None, "prow", "pcol", None),
        P(None, "prow", None, None, "pcol", None),
    )
    return jax.shard_map(body, mesh=mesh, in_specs=in_specs, out_specs=out_specs, check_vma=False)
```

profile of v0, /device:TPU:0, one launch (start us, length us, event | category | flops | bytes accessed | tf_op | source)
XLA Modules:
  0.0 531.9 jit_solution(17164543631338080142)
XLA Ops:
  7.2 0.0 copy-start
  7.2 0.0 all-gather.5.cloned.1.call-start
  7.2 0.7 all-gather.5.cloned.1.call-update
  7.9 0.0 all-gather.7.cloned.1.call-start
  8.0 51.2 %all-gather.5.cloned.1.call-done = f32[1024,1024]{1,0:T(8,128)} async-done(((f32[128,1024]{1,0:T(8,128)}), f32[1024,1024]{1,0:T(8,128)}) %all-gather.5.cloned.1.call-update) | async-done | bytes 4194320 | tf_op jit(solution)/shard_map/all_gather | solution.py:20
  59.2 7.5 %fusion.15 = f32[128,1024]{1,0:T(8,128)} fusion(f32[128,1024]{1,0:T(8,128)} %param.6, f32[1024,1024]{1,0:T(8,128)} %all-gather.5.cloned.1.call-done), kind=kOutput, calls=%fused_computation.21 | convolution fusion | flops 1610612736 | bytes 5242880 | tf_op jit(solution)/shard_map/dot_general | solution.py:21
  66.7 0.0 all-gather.7.cloned.1.call-update
  66.8 0.0 all-gather.11.cloned.1.call-start
  66.8 0.7 all-gather.11.cloned.1.call-update
  67.5 0.0 copy-start.5
  67.5 0.0 all-gather.9.cloned.1.call-start
  67.6 45.0 %all-gather.7.cloned.1.call-done = f32[1024,1024]{1,0:T(8,128)} async-done(((f32[128,1024]{1,0:T(8,128)}), f32[1024,1024]{1,0:T(8,128)}) %all-gather.7.cloned.1.call-update) | async-done | bytes 4194320 | tf_op jit(solution)/shard_map/all_gather | solution.py:24
  112.6 30.4 %fusion.16 = f32[1024,1024]{1,0:T(8,128)S(1)} fusion(f32[1024,1024]{1,0:T(8,128)} %all-gather.7.cloned.1.call-done, f32[1024,1024]{1,0:T(8,128)} %all-gather.5.cloned.1.call-done), kind=kOutput, calls=%fused_computation.22 | convolution fusion | flops 12884901888 | bytes 12582912 | tf_op jit(solution)/shard_map/dot_general | solution.py:25
  143.0 0.0 copy-start.3
  143.0 0.0 copy-start.2
  143.0 0.0 copy-done.5
  143.0 3.8 fusion.13
  146.9 0.0 copy-done
  146.9 0.0 copy-done.2
  146.9 5.1 fusion.14
  152.0 0.0 copy-done.3
  152.0 0.0 all-gather.9.cloned.1.call-update
  152.0 0.0 all-reduce.3.cloned.1.call-start
  152.1 43.0 %all-gather.11.cloned.1.call-done = f32[16,1,128,1024]{3,2,0,1:T(8,128)} async-done(((f32[16,1,16,1024]{3,2,0,1:T(8,128)}), f32[16,1,128,1024]{3,2,0,1:T(8,128)}) %all-gather.11.cloned.1.call-update) | async-done | bytes 8388624 | tf_op jit(solution)/shard_map/all_gather | solution.py:44
  195.1 5.0 fusion.6
  200.1 77.0 %all-gather.9.cloned.1.call-done = f32[16,1,128,1024]{3,2,0,1:T(8,128)} async-done(((f32[16,1,16,1024]{3,2,0,1:T(8,128)}), f32[16,1,128,1024]{3,2,0,1:T(8,128)}) %all-gather.9.cloned.1.call-update) | async-done | bytes 8388624 | tf_op jit(solution)/shard_map/all_gather | solution.py:43
  277.1 5.0 fusion.5
  282.0 0.0 all-reduce.3.cloned.1.call-update
  282.1 0.1 broadcast_compare_fusion
  282.2 1.1 dynamic-slice_bitcast_fusion
  283.3 1.0 copy.19
  284.3 168.5 %all-reduce.3.cloned.1.call-done = (f32[8,128,1024]{2,1,0:T(8,128)}, f32[8,128,1024]{2,1,0:T(8,128)}) async-done(((f32[8,128,1024]{2,1,0:T(8,128)}, f32[8,128,1024]{2,1,0:T(8,128)}), (f32[8,128,1024]{2,1,0:T(8,128)}, f32[8,128,1024]{2,1,0:T(8,128)})) %all-reduce.3.cloned.1.call-update) | async-done | bytes 8388624 | tf_op jit(solution)/shard_map/psum | solution.py:9
  452.8 0.0 copy-start.4
  452.8 30.9 %fusion.3 = f32[16,128,8,128]{3,1,2,0:T(8,128)S(1)} fusion(f32[16,1,128,1024]{3,2,0,1:T(8,128)} %all-gather.9.cloned.1.call-done, f32[8,128,1024]{2,1,0:T(8,128)} %get-tuple-element.9), kind=kOutput, calls=%fused_computation.4 | convolution fusion | flops 25769803776 | bytes 20971520 | tf_op jit(solution)/shard_map/isk,jtk->isjt/dot_general | solution.py:66
  483.7 0.0 copy-done.4
  483.7 31.5 %fusion = f32[16,1,128,8,1,128]{5,2,3,0,4,1:T(8,128)S(1)} fusion(f32[16,128,8,128]{3,1,2,0:T(8,128)S(1)} %fusion.3, f32[16,1,128,8,1,128]{5,4,3,2,1,0:T(1,128)} %param.9, pred[16,8]{1,0:T(8,128)(4,1)S(1)} %broadcast_compare_fusion, f32[16,1,128,1024]{3,2,0,1:T(8,128)} %all-gather.11.cloned.1.call-done, f32[8,128,1024]{2,1,0:T(8,128)S(1)} %copy-done.4), kind=kOutput, calls=%fused_computation.1 | convolution fusion | flops 25776095232 | bytes 37748864 | tf_op jit(solution)/shard_map/isk,jtk->isjt/dot_general | solution.py:69
  515.2 0.0 copy-start.1
  515.2 9.8 %copy.21 = f32[16,1,128,8,1,128]{5,4,3,2,1,0:T(1,128)} copy(f32[16,1,128,8,1,128]{5,2,3,0,4,1:T(8,128)S(1)} %fusion) | data formatting | bytes 16777216
  525.1 0.0 copy-done.1
  (2 shorter events, 0.0 us)
Async XLA Ops:
  7.2 139.7 %copy-start = (f32[16,1,16,1024]{3,2,1,0:T(8,128)S(1)}, f32[16,1,16,1024]{3,2,1,0:T(8,128)}, u32[]{:S(2)}) copy-start(f32[16,1,16,1024]{3,2,1,0:T(8,128)} %param.7) | copy-start | bytes 3145732
  7.2 52.0 %all-gather.5.cloned.1.call-start = ((), (), s32[]{:S(2)}) async-start(), calls=%async_computation | async-start | bytes 4718592 | tf_op jit(solution)/shard_map/all_gather | solution.py:20
  7.9 104.7 %all-gather.7.cloned.1.call-start = ((), (), s32[]{:S(2)}) async-start(), calls=%async_computation.1 | async-start | bytes 4718592 | tf_op jit(solution)/shard_map/all_gather | solution.py:24
  66.8 128.3 %all-gather.11.cloned.1.call-start = ((), (), s32[]{:S(2)}) async-start(), calls=%async_computation.3 | async-start | bytes 9437184 | tf_op jit(solution)/shard_map/all_gather | solution.py:44
  67.5 75.5 %copy-start.5 = (f32[16,1,16,1024]{3,2,1,0:T(8,128)S(1)}, f32[16,1,16,1024]{3,2,1,0:T(8,128)}, u32[]{:S(2)}) copy-start(f32[16,1,16,1024]{3,2,1,0:T(8,128)} %param.8) | copy-start | bytes 3145732
  67.5 209.6 %all-gather.9.cloned.1.call-start = ((), (), s32[]{:S(2)}) async-start(), calls=%async_computation.2 | async-start | bytes 9437184 | tf_op jit(solution)/shard_map/all_gather | solution.py:43
  143.0 9.0 %copy-start.3 = (f32[1024,1024]{1,0:T(8,128)}, f32[1024,1024]{1,0:T(8,128)S(1)}, u32[]{:S(2)}) copy-start(f32[1024,1024]{1,0:T(8,128)S(1)} %fusion.16) | copy-start | bytes 12582916
  143.0 3.9 copy-start.2
  152.0 300.8 %all-reduce.3.cloned.1.call-start = ((), (), s32[]{:S(2)}) async-start(), calls=%async_computation.4 | async-start | bytes 16777216 | tf_op jit(solution)/shard_map/psum | solution.py:9
  452.8 30.9 %copy-start.4 = (f32[8,128,1024]{2,1,0:T(8,128)S(1)}, f32[8,128,1024]{2,1,0:T(8,128)}, u32[]{:S(2)}) copy-start(f32[8,128,1024]{2,1,0:T(8,128)} %get-tuple-element.10) | copy-start | bytes 12582916
  515.2 9.8 %copy-start.1 = (f32[16,1,16,1024]{3,2,1,0:T(8,128)S(1)}, f32[16,1,16,1024]{3,2,1,0:T(8,128)}, u32[]{:S(2)}) copy-start(f32[16,1,16,1024]{3,2,1,0:T(8,128)} %param.7) | copy-start | bytes 3145732
Sparse Core Ops, SparseCore 0:
  9.6 49.5 all-gather.4
  66.9 45.6 all-gather.6
  114.2 80.8 all-gather.10
  196.5 80.5 all-gather.8
  282.2 170.5 all-reduce.2
where the time goes:
time: 535 us; the launch traced here: 532 us
  waiting for transfers between devices  386 us (72%)
  matrix products  109 us (20%)
  between operations  14.2 us (3%)
  local copies, waits for them, and re-layouts  11.9 us (2%)
  other arithmetic  10 us (2%)
    psum x1, waiting for transfers between devices, broadcast(): return lax.psum(jnp.where(mine, array, jnp.zeros_like(array)), axis)  169 us
    all_gather x1, waiting for transfers between devices, body(): lax.all_gather(shifted.reshape(shape), 'pcol', axis=2, tiled=True)  77 us
    all_gather x1, waiting for transfers between devices, body(): inverse_full = lax.all_gather(inverse_factor, 'pcol', axis=0, tiled=True)  51.2 us
    all_gather x1, waiting for transfers between devices, body(): terms_full = lax.all_gather(diag_terms, 'pcol', axis=0, tiled=True)  45 us
    all_gather x1, waiting for transfers between devices, body(): lax.all_gather(panel_factor, 'pcol', axis=2, tiled=True)  43 us
    dot_general x1, matrix products, body(): jnp.einsum('isk,jtk->isjt', rows_l, col_y, precision=exact, preferred_ele...  31.5 us
    dot_general x1, matrix products, body(): jnp.einsum('isk,jtk->isjt', rows_y, col_l, precision=exact, preferred_ele...  30.9 us
    dot_general x1, matrix products, body(): jnp.dot(inverse_full, terms_full, precision=exact, preferred_element_type...  30.4 us
  transfers between devices with their start and end apart: 5, of which 5 were waited for; matrix products, arithmetic and copies ran while one was open for 9% of the time, Pallas kernels for 0%

commit v1 on v0

v1 whole, which is shorter than its diff:
```python
import functools

import jax
import jax.numpy as jnp
from jax import lax
from jax.experimental import pallas as pl
from jax.experimental.pallas import tpu as pltpu
from jax.sharding import PartitionSpec as P

AXES = ("prow", "pcol")
WHOLE_LIMIT = 40 * 2**20


def split(x):
    high = x.astype(jnp.bfloat16)
    low = (x - high.astype(jnp.float32)).astype(jnp.bfloat16)
    return high, low


def dot(a, b):
    return jnp.dot(a, b, precision=lax.Precision.HIGH, preferred_element_type=jnp.float32)


def mul_t(a, b):
    return lax.dot_general(a, b, (((1,), (1,)), ((), ())), preferred_element_type=jnp.float32)


def update_kernel(
    grid_rows, grid_cols, group, wide, ids,
    rows_y, rows_f, cols_y, cols_f, old, new,
    ry_h, ry_l, rf_h, rf_l, cy_h, cy_l, cf_h, cf_l,
):
    step = pl.program_id(0)
    col_tiles = cols_y.shape[2]
    tile = old.shape[1]

    @pl.when(step == 0)
    def _():
        for source, high, low in ((cols_y, cy_h, cy_l), (cols_f, cf_h, cf_l)):
            @pl.loop(0, col_tiles)
            def _(j):
                h, l = split(source[0, :, j, 0].reshape(tile, -1))
                at = pl.ds(pl.multiple_of(j * tile, tile), tile)
                high[at, :] = h
                low[at, :] = l

    for source, high, low in ((rows_y, ry_h, ry_l), (rows_f, rf_h, rf_l)):
        @pl.loop(0, group)
        def _(i):
            h, l = split(source[0, :, i].reshape(tile, -1))
            at = pl.ds(pl.multiple_of(i * tile, tile), tile)
            high[at, :] = h
            low[at, :] = l
    new[...] = old[...]
    span = wide * tile
    last = (step * group + group - 1) * grid_rows + grid_rows - 1
    count = lax.min(last // (grid_cols * wide) + 1, col_tiles // wide)

    for b in range(col_tiles // wide):
        @pl.when(b < count)
        def _():
            at = pl.ds(b * span, span)
            fh, yh = cf_h[at, :], cy_h[at, :]
            total = mul_t(ry_h[...], fh) + mul_t(ry_l[...], fh) + mul_t(ry_h[...], cf_l[at, :])
            total += mul_t(rf_h[...], yh) + mul_t(rf_l[...], yh) + mul_t(rf_h[...], cy_l[at, :])
            for i in range(group):
                row = (step * group + i) * grid_rows + ids[0]
                for w in range(wide):
                    j = b * wide + w
                    @pl.when(row >= j * grid_cols + ids[1])
                    def _():
                        part = total[i * tile:(i + 1) * tile, w * tile:(w + 1) * tile]
                        new[i, :, j, :] = old[i, :, j, :] - part


def spread(x, tile_rows, col_tiles):
    grid_rows, grid_cols = lax.axis_size("prow"), lax.axis_size("pcol")
    column, row = lax.axis_index("pcol"), lax.axis_index("prow")
    stride = grid_cols // grid_rows
    piece, width = x.shape[0] // tile_rows, x.shape[1]
    root, picked = column % grid_rows, column // grid_rows
    by_row = (-1, grid_cols, tile_rows, piece, width)
    by_col = (-1, grid_cols, col_tiles, stride, piece, width)
    if x.size * 4 * grid_rows * grid_cols <= WHOLE_LIMIT:
        everything = lax.all_gather(x, AXES, axis=0, tiled=False)
        return everything.reshape(by_row), everything.reshape(by_col), (row, root, picked)
    rows = lax.all_gather(x, "pcol", axis=0, tiled=False)
    cols = lax.dynamic_index_in_dim(rows.reshape(by_col), picked, 3, keepdims=True)
    cols = lax.psum(jnp.where(row == root, cols, jnp.zeros_like(cols)), "prow")
    return rows.reshape(by_row), cols, (0, 0, 0)


def update(y_parts, f_parts, trailing):
    grid_rows, grid_cols = lax.axis_size("prow"), lax.axis_size("pcol")
    tile_rows, tile, col_tiles = trailing.shape[0], trailing.shape[2], trailing.shape[3]
    y_rows, y_cols, places = y_parts
    f_rows, f_cols, _ = f_parts
    piece, width = y_rows.shape[-2:]
    column, row = lax.axis_index("pcol"), lax.axis_index("prow")
    ids = jnp.stack([jnp.int32(v) for v in (row, column) + places])
    group = 4 if tile_rows % 4 == 0 else 1
    wide = 2 if col_tiles % 2 == 0 else 1
    rows = pl.BlockSpec((1, grid_cols, group, piece, width), lambda s, d: (d[2], 0, s, 0, 0))
    cols = pl.BlockSpec(
        (1, grid_cols, col_tiles, 1, piece, width), lambda s, d: (d[3], 0, 0, d[4], 0, 0),
        pipeline_mode=pl.Buffered(1),
    )
    block = pl.BlockSpec((group, tile, col_tiles, tile), lambda s, d: (s, 0, 0, 0))
    row_scratch = pltpu.VMEM((group * tile, width), jnp.bfloat16)
    col_scratch = pltpu.VMEM((col_tiles * tile, width), jnp.bfloat16)
    old = trailing.reshape(tile_rows, tile, col_tiles, tile)
    new = pl.pallas_call(
        functools.partial(update_kernel, grid_rows, grid_cols, group, wide),
        out_shape=jax.ShapeDtypeStruct(old.shape, jnp.float32),
        grid_spec=pltpu.PrefetchScalarGridSpec(
            num_scalar_prefetch=1, grid=(tile_rows // group,),
            in_specs=[rows, rows, cols, cols, block], out_specs=block,
            scratch_shapes=[row_scratch] * 4 + [col_scratch] * 4,
        ),
        compiler_params=pltpu.CompilerParams(vmem_limit_bytes=60 * 2**20),
    )(
        ids, y_rows, f_rows, y_cols, f_cols, old,
    )
    return new.reshape(trailing.shape)


def body(inverse_factor, diag_block, panel_matrix, panel_factor, trailing):
    grid_rows, grid_cols = lax.axis_size("prow"), lax.axis_size("pcol")
    row = lax.axis_index("prow")
    local, width = inverse_factor.shape
    share = local // grid_rows
    both = jnp.stack([
        lax.dynamic_slice_in_dim(inverse_factor, row * share, share, 0),
        lax.dynamic_slice_in_dim(diag_block, row * share, share, 0),
    ])
    both = lax.all_gather(both, AXES, axis=0, tiled=False)
    both = both.reshape(grid_rows, grid_cols, 2, share, width).transpose(2, 1, 0, 3, 4)
    inverse, diag = both.reshape(2, grid_cols * local, width)
    factor = panel_factor.reshape(-1, width)
    sizes = trailing.shape[0], trailing.shape[3]
    f_parts = spread(factor, *sizes)
    panel = panel_matrix.reshape(-1, width)
    mid = dot(dot(factor, inverse), diag)
    shifted = dot(panel - 0.5 * mid, inverse.T)
    y_parts = spread(shifted, *sizes)
    panel_result = dot(panel - mid, inverse.T).reshape(panel_matrix.shape)
    reduced = dot(dot(inverse_factor, diag), inverse.T)
    return reduced, panel_result, update(y_parts, f_parts, trailing)


def solution(mesh):
    in_specs = (
        P("pcol", None),
        P("pcol", None),
        P(None, "prow", "pcol", None),
        P(None, "prow", "pcol", None),
        P(None, "prow", None, None, "pcol", None),
    )
    out_specs = (
        P("pcol", None),
        P(None, "prow", "pcol", None),
        P(None, "prow", None, None, "pcol", None),
    )
    return jax.shard_map(body, mesh=mesh, in_specs=in_specs, out_specs=out_specs, check_vma=False)
```

time: 535 us -> 526 us (0.983)
  matrix products: 109 us -> 20.5 us
  waiting for transfers between devices: 386 us -> 446 us
  Pallas kernels: 0 us -> 36.2 us
  other arithmetic: 10 us -> 0.72 us
    all_gather x4 -> x3, waiting for transfers between devices: 216 us -> 445 us  [the longest x2 363 us: spread(): everything = lax.all_gather(x, AXES, axis=0, tiled=False)]
    psum x1 -> x0, waiting for transfers between devices: 169 us -> none  [broadcast(): return lax.psum(jnp.where(mine, array, jnp.zeros_like(array)), axis)]
    dot_general x6, matrix products: 109 us -> 20.5 us  [dot(): jnp.dot(a, b, precision=lax.Precision.HIGH, preferred_element_type=jnp.fl...]
    pallas_call x0 -> x1, Pallas kernels: none -> 36.2 us  [update(): pl.pallas_call(functools.partial(update_kernel, grid_rows, grid_cols, gro...]
    select_n x2 -> x0, other arithmetic: 9.94 us -> none  [broadcast(): return lax.psum(jnp.where(mine, array, jnp.zeros_like(array)), axis)]
    unnamed x14, local copies, waits for them, and re-layouts: 10.9 us -> 1.45 us
    another operation x0 -> x5, local copies, waits for them, and re-layouts: none -> 6.96 us  [the longest x3 5.37 us: body(): inverse, diag = both.reshape(2, grid_cols * local, width)]
  transfers between devices with their start and end apart: 5 -> 3, of which waited for: 5 -> 3; matrix products, arithmetic and copies ran while one was open for 9% -> 5% of each run, Pallas kernels for 0% -> 0%
where the time goes in v1:
time: 526 us; the launch traced here: 525 us
  waiting for transfers between devices  446 us (85%)
  Pallas kernels  36.2 us (7%)
  matrix products  20.5 us (4%)
  between operations  13.9 us (3%)
  local copies, waits for them, and re-layouts  8.4 us (2%)
    all_gather x2, waiting for transfers between devices, spread(): everything = lax.all_gather(x, AXES, axis=0, tiled=False)  363 us
    all_gather x1, waiting for transfers between devices, body(): both = lax.all_gather(both, AXES, axis=0, tiled=False)  81.6 us
    pallas_call x1, Pallas kernels, update(): pl.pallas_call(functools.partial(update_kernel, grid_rows, grid_cols, gro...  36.2 us
    dot_general x6, matrix products, dot(): jnp.dot(a, b, precision=lax.Precision.HIGH, preferred_element_type=jnp.fl...  20.5 us
  transfers between devices with their start and end apart: 3, of which 3 were waited for; matrix products, arithmetic and copies ran while one was open for 5% of the time, Pallas kernels for 0%

profile of v1, /device:TPU:0, one launch (start us, length us, event | category | flops | bytes accessed | tf_op | source)
XLA Modules:
  0.0 525.3 jit_solution(12877210039795518665)
XLA Ops:
  7.2 0.0 all-gather.8.cloned.1.call-start
  7.2 1.0 dynamic-slice_bitcast_fusion
  8.2 0.7 pad_maximum_fusion
  8.9 0.0 all-gather.8.cloned.1.call-update
  9.0 0.0 all-gather.6.cloned.1.call-start
  9.0 0.7 all-gather.6.cloned.1.call-update
  9.7 0.0 all-gather.10.cloned.1.call-start
  9.8 81.6 %all-gather.8.cloned.1.call-done = f32[64,32,1024]{2,1,0:T(8,128)} async-done(((f32[2,32,1024]{2,1,0:T(8,128)}), f32[64,32,1024]{2,1,0:T(8,128)}) %all-gather.8.cloned.1.call-update) | async-done | bytes 8388624 | tf_op jit(solution)/shard_map/all_gather | solution.py:136
  91.4 4.3 fusion
  95.7 0.5 copy.18
  96.2 0.0 copy-start
  96.2 0.0 copy-start.4
  96.2 0.5 copy.17
  96.8 0.0 copy-start.2
  96.8 0.0 copy-start.5
  96.8 1.4 copy-done.4
  98.2 3.4 fusion.3
  101.6 0.0 copy-done.5
  101.7 2.0 bitcast_subtract_fusion
  103.7 0.0 copy-done.2
  103.7 0.0 copy-done
  103.7 2.9 fusion.4
  106.6 0.0 copy-start.6
  106.6 0.0 all-gather.10.cloned.1.call-update
  106.7 0.6 stack.32.ids
  107.3 0.0 copy-start.3
  107.3 5.2 convolution_bitcast_fusion
  112.5 0.0 copy-done.6
  112.5 0.0 copy-done.3
  112.5 0.0 copy-start.1
  112.5 3.7 fusion.1
  116.2 0.0 copy-done.1
  116.2 3.2 fusion.2
  119.4 167.8 %all-gather.6.cloned.1.call-done = f32[32,256,1024]{2,1,0:T(8,128)} async-done(((f32[1,256,1024]{2,1,0:T(8,128)}), f32[32,256,1024]{2,1,0:T(8,128)}) %all-gather.6.cloned.1.call-update) | async-done | bytes 33554448 | tf_op jit(solution)/shard_map/all_gather | solution.py:85
  287.2 195.4 %all-gather.10.cloned.1.call-done = f32[8192,1024]{1,0:T(8,128)} async-done(((f32[256,1024]{1,0:T(8,128)}), f32[8192,1024]{1,0:T(8,128)}) %all-gather.10.cloned.1.call-update) | async-done | bytes 33554448 | tf_op jit(solution)/shard_map/all_gather | solution.py:85
  482.6 36.2 %shard_map.76 = f32[16,128,8,128]{3,2,1,0:T(8,128)} custom-call(s32[5]{0:T(128)} %stack.32.ids, f32[4,8,16,16,1024]{4,3,2,1,0:T(8,128)} %bitcast.47, f32[4,8,16,16,1024]{4,3,2,1,0:T(8,128)} %bitcast.45, f32[4,8,8,2,16,1024]{5,4,3,2,1,0:T(8,128)} %bitcast.48, f32[4,8,8,2,16,1024]{5,4,3,2,1,0:T(8,128)} %bitcast.46, f32[16,128,8,128]{3,2,1,0:T(8,128)} %bitcast.55), custom_call_target="tpu_custom_call" | custom-call | tf_op jit(solution)/shard_map/pallas_call | solution.py:112
Async XLA Ops:
  7.2 84.2 %all-gather.8.cloned.1.call-start = ((), (), s32[]{:S(2)}) async-start(), calls=%async_computation.1 | async-start | bytes 8650752 | tf_op jit(solution)/shard_map/all_gather | solution.py:136
  9.0 278.2 %all-gather.6.cloned.1.call-start = ((), (), s32[]{:S(2)}) async-start(), calls=%async_computation | async-start | bytes 34603008 | tf_op jit(solution)/shard_map/all_gather | solution.py:85
  9.7 472.8 %all-gather.10.cloned.1.call-start = ((), (), s32[]{:S(2)}) async-start(), calls=%async_computation.2 | async-start | bytes 34603008 | tf_op jit(solution)/shard_map/all_gather | solution.py:85
  96.2 7.5 %copy-start = (f32[1,8,4,32,1024]{4,3,2,1,0:T(8,128)}, f32[1,8,4,32,1024]{4,3,2,1,0:T(8,128)S(1)}, u32[]{:S(2)}) copy-start(f32[1,8,4,32,1024]{4,3,2,1,0:T(8,128)S(1)} %copy.18) | copy-start | bytes 12582916
  96.2 2.0 copy-start.4
  96.8 6.9 %copy-start.2 = (f32[1,8,4,32,1024]{4,3,2,1,0:T(8,128)}, f32[1,8,4,32,1024]{4,3,2,1,0:T(8,128)S(1)}, u32[]{:S(2)}) copy-start(f32[1,8,4,32,1024]{4,3,2,1,0:T(8,128)S(1)} %copy.17) | copy-start | bytes 12582916
  96.8 4.9 copy-start.5
  106.6 5.9 %copy-start.6 = (f32[128,1024]{1,0:T(8,128)S(1)}, f32[128,1024]{1,0:T(8,128)}, u32[]{:S(2)}) copy-start(f32[128,1024]{1,0:T(8,128)} %param.5) | copy-start | bytes 1572868
  107.3 5.2 copy-start.3
  112.5 3.7 copy-start.1
Sparse Core Ops, SparseCore 0:
  11.5 79.7 all-gather.7
  94.3 192.7 all-gather.5
  290.2 192.3 all-gather.9
